TPU v7x, 32 devices: a whole 2x2x4 slice. The times are simulated.
32 devices in a mesh: outer: 2 (over core), inner: 16 (over z, y, x).
Axes of the slice: x: 2, y: 2, z: 4, core: 2. Of those that a mesh axis runs over, the one named last changes fastest.
Arguments:
- inputs: float32 [50176, 256], P(('outer', 'inner')), may hold values from -6 to 6
- cotangent: float32 [50176, 1024], P(('outer', 'inner')), may hold values from -200 to 200
- weight: float32 [1024, 256], replicated, may hold values from -0.375 to 0.375
- momentum: float32 [1024, 256], P('inner', 'outer'), may hold values from -4 to 4
Outputs:
- input_grad: float32 [50176, 256], P(('outer', 'inner'))
- new_weight: float32 [1024, 256], P(None, 'outer')
- new_momentum: float32 [1024, 256], P('inner', 'outer')
All inputs are finite; a program needn't handle non-finite values.
Results may differ from a plain program's by a relative error of at most 0.0001.
Values sent between devices are 32-bit elements; how exact they have to be, the bound alone decides.
A program may use at most 64 MiB of HBM per device.

v0:
```python
import jax
import jax.numpy as jnp
from jax import lax
from jax.sharding import PartitionSpec as P

HIGH = lax.Precision.HIGHEST


def partner_2(value, axis, bit):
    mask = 2**bit
    pairs = [(source, source ^ mask) for source in range(lax.axis_size(axis))]
    return lax.ppermute(value, axis, pairs)


def combine_pair(first, second, cross, first_sq, second_sq):
    return (1.0 - cross / (2.0 * (first_sq + 1e-06))) * first + (
        1.0 - cross / (2.0 * (second_sq + 1e-06))
    ) * second


def partner(shard, level):
    return partner_2(shard, "outer", level)


def combine_level(shard, level):
    other = partner(shard, level)
    cross, first_sq, second_sq = lax.psum(
        (jnp.sum(shard * other), jnp.sum(shard * shard), jnp.sum(other * other)), "inner"
    )
    return combine_pair(shard, other, cross, first_sq, second_sq)


def per_device(inputs, cotangent, weight, momentum):
    pre = lax.dot_general(
        inputs, weight, (((1,), (1,)), ((), ())), precision=HIGH, preferred_element_type=jnp.float32
    )
    sig = jax.nn.sigmoid(pre)
    slope = cotangent * (sig * (1.0 + pre * (1.0 - sig)))
    scale = 1.0 / (inputs.shape[0] * lax.axis_size("inner"))
    shard_rows = momentum.shape[0]
    own_width = momentum.shape[1]
    col_start = lax.axis_index("outer") * own_width
    product = lax.dot_general(
        slope, inputs, (((0,), (0,)), ((), ())), precision=HIGH, preferred_element_type=jnp.float32
    )
    shard = lax.psum_scatter(product * scale, "inner", scatter_dimension=0, tiled=True)
    input_grad = jnp.dot(slope, weight, precision=HIGH, preferred_element_type=jnp.float32)
    weight_cols = lax.dynamic_slice_in_dim(weight, col_start, own_width, 1)
    shard = combine_level(shard, 0)
    new_momentum = 0.9 * momentum + lax.dynamic_slice_in_dim(shard, col_start, own_width, 1)
    own_rows = lax.dynamic_slice_in_dim(
        weight_cols, lax.axis_index("inner") * shard_rows, shard_rows, 0
    )
    new_weight = lax.all_gather(own_rows - 0.1 * new_momentum, "inner", axis=0, tiled=True)
    return (input_grad, new_weight, new_momentum)


def solution(mesh):
    placed = (P(("outer", "inner"), None), P(("outer", "inner"), None), P(), P("inner", "outer"))
    return jax.shard_map(
        per_device,
        mesh=mesh,
        in_specs=placed,
        out_specs=(P(("outer", "inner"), None), P(None, "outer"), P("inner", "outer")),
        check_vma=False,
    )
```

profile of v0, /device:TPU:0, one launch (start us, length us, event | category | flops | bytes accessed | tf_op | source)
XLA Modules:
  0.0 212.0 jit_solution(7491985779900272858)
XLA Ops:
  7.2 0.0 copy-start
  7.2 0.0 reduce-scatter.2.cloned.1.call-start
  7.2 1.4 copy-done
  8.6 9.6 %multiply_multiply_fusion = f32[1568,1024]{1,0:T(8,128)S(1)} fusion(f32[1568,1024]{1,0:T(8,128)} %param.5, f32[1568,256]{1,0:T(8,128)S(1)} %copy-done, f32[1024,256]{1,0:T(8,128)} %param.6), kind=kOutput, calls=%fused_computation | convolution fusion | flops 4945346560 | bytes 15499264 | tf_op jit(solution)/shard_map/dot_general | solution.py:34
  18.2 0.0 copy-start.1
  18.2 2.7 %copy-done.1 = f32[1568,1024]{1,0:T(8,128)} copy-done((f32[1568,1024]{1,0:T(8,128)}, f32[1568,1024]{1,0:T(8,128)S(1)}, u32[]{:S(2)}) %copy-start.1) | copy-done | bytes 6422552
  20.9 0.0 copy-start.2
  20.9 11.7 %convolution_multiply_fusion = f32[1024,256]{1,0:T(8,128)} fusion(f32[1568,1024]{1,0:T(8,128)S(1)} %multiply_multiply_fusion, f32[1568,256]{1,0:T(8,128)S(1)} %copy-done), kind=kOutput, calls=%fused_computation.1 | convolution fusion | flops 4932763648 | bytes 9076736 | tf_op jit(solution)/shard_map/dot_general | solution.py:43
  32.6 0.0 reduce-scatter.2.cloned.1.call-update
  32.6 0.0 copy-start.4
  32.6 81.5 %reduce-scatter.2.cloned.1.call-done = f32[64,256]{1,0:T(8,128)} async-done(((f32[1024,256]{1,0:T(8,128)}), f32[64,256]{1,0:T(8,128)}) %reduce-scatter.2.cloned.1.call-update) | async-done | bytes 65552 | tf_op jit(solution)/shard_map/reduce_scatter | solution.py:46
  114.2 0.0 copy-start.3
  114.2 0.0 collective-permute-start
  114.2 0.0 copy-done.2
  114.2 8.4 %fusion.3 = f32[1568,256]{1,0:T(8,128)} fusion(f32[1568,1024]{1,0:T(8,128)} %copy-done.1, f32[1024,256]{1,0:T(8,128)S(1)} %copy-done.2), kind=kOutput, calls=%fused_computation.10 | convolution fusion | flops 4932501504 | bytes 9076736 | tf_op jit(solution)/shard_map/dot_general | solution.py:47
  122.5 0.0 collective-permute-done
  122.5 0.0 copy-done.3
  122.5 0.7 multiply_reduce_fusion.1
  123.2 37.8 %all-reduce = (f32[]{:T(128)}, f32[]{:T(128)}, f32[]{:T(128)}) all-reduce(f32[]{:T(128)} %get-tuple-element.4, f32[]{:T(128)} %get-tuple-element.5, f32[]{:T(128)} %get-tuple-element.3), channel_id=1, replica_groups=mesh['outer'=2,'inner'=16] {'inner'}, use_global_device_ids=true, to_apply=%region_2.0 | all-reduce | flops 3 | bytes 24 | tf_op jit(solution)/shard_map/psum | solution.py:27
  163.6 0.0 copy-done.4
  163.6 0.6 multiply_subtract_fusion
  164.2 40.1 %all_gather.3 = f32[1024,128]{1,0:T(8,128)S(1)} all-gather(f32[64,128]{1,0:T(8,128)S(1)} %get-tuple-element.9), channel_id=1, replica_groups=mesh['outer'=2,'inner'=16] {'inner'}, dimensions={0}, use_global_device_ids=true | all-gather | bytes 557056 | tf_op jit(solution)/shard_map/all_gather | solution.py:54
  204.3 0.8 copy.8
Async XLA Ops:
  7.2 1.4 copy-start
  7.2 107.0 %reduce-scatter.2.cloned.1.call-start = ((), (), s32[]{:S(2)}) async-start(), calls=%async_computation.1 | async-start | bytes 1114112 | tf_op jit(solution)/shard_map/reduce_scatter | solution.py:46
  18.2 2.7 %copy-start.1 = (f32[1568,1024]{1,0:T(8,128)}, f32[1568,1024]{1,0:T(8,128)S(1)}, u32[]{:S(2)}) copy-start(f32[1568,1024]{1,0:T(8,128)S(1)} %multiply_multiply_fusion) | copy-start | bytes 19267588
  20.9 93.3 %copy-start.2 = (f32[1024,256]{1,0:T(8,128)S(1)}, f32[1024,256]{1,0:T(8,128)}, u32[]{:S(2)}) copy-start(f32[1024,256]{1,0:T(8,128)} %param.6) | copy-start | bytes 3145732
  32.6 131.0 %copy-start.4 = (f32[64,128]{1,0:T(8,128)S(1)}, f32[64,128]{1,0:T(8,128)}, u32[]{:S(2)}) copy-start(f32[64,128]{1,0:T(8,128)} %param.7) | copy-start | bytes 98308
  114.2 8.4 %copy-start.3 = (f32[64,256]{1,0:T(8,128)S(1)}, f32[64,256]{1,0:T(8,128)}, u32[]{:S(2)}) copy-start(f32[64,256]{1,0:T(8,128)} %reduce-scatter.2.cloned.1.call-done) | copy-start | bytes 196612
  114.2 8.4 %collective-permute-start = (f32[64,256]{1,0:T(8,128)}, f32[64,256]{1,0:T(8,128)S(1)}, u32[]{:S(2)}, u32[]{:S(2)}) collective-permute-start(f32[64,256]{1,0:T(8,128)} %reduce-scatter.2.cloned.1.call-done), channel_id=1, source_target_pairs={{0,16},{16,0},{1,17},{17,1},{2,18},{18,2},{3,19},{19,3},{4,20},{20... | collective-permute-start | bytes 196616 | tf_op jit(solution)/shard_map/ppermute | solution.py:12
Sparse Core Ops, SparseCore 0:
  32.7 81.3 reduce-scatter.1
where the time goes:
time: 212 us
  waiting for transfers between devices  81.6 us (38%)
  blocking collectives  77.9 us (37%)
  matrix products  29.7 us (14%)
  between operations  16.6 us (8%)
  local copies, waits for them, and re-layouts  4.87 us (2%)
    reduce_scatter x1, waiting for transfers between devices, per_device(): lax.psum_scatter(product * scale, 'inner', scatter_dimension=0, tiled=True)  81.5 us
    all_gather x1, blocking collectives, per_device(): lax.all_gather(own_rows - 0.1 * new_momentum, 'inner', axis=0, tiled=True)  40.1 us
    psum x1, blocking collectives, combine_level(): lax.psum((jnp.sum(shard * other), jnp.sum(shard * shard), jnp.sum(other *...  37.8 us
    dot_general x1, matrix products, per_device(): lax.dot_general(slope, inputs, (((0,), (0,)), ((), ())), precision=HIGH,...  11.7 us
    dot_general x1, matrix products, per_device(): lax.dot_general(inputs, weight, (((1,), (1,)), ((), ())), precision=HIGH,...  9.57 us
    dot_general x1, matrix products, per_device(): jnp.dot(slope, weight, precision=HIGH, preferred_element_type=jnp.float32)  8.35 us
    unnamed x11, local copies, waits for them, and re-layouts  4.87 us
  transfers between devices with their start and end apart: 2, of which 1 were waited for; matrix products, arithmetic and copies ran while one was open for 4% of the time, Pallas kernels for 0%

commit v1 on v0

v1 whole, which is shorter than its diff:
```python
import functools

import jax
import jax.numpy as jnp
from jax import lax
from jax.experimental import pallas as pl
from jax.experimental.pallas import tpu as pltpu
from jax.sharding import PartitionSpec as P

MESH = pl.DeviceIdType.MESH
F32 = jnp.float32
BF16 = jnp.bfloat16


def split(value):
    high = value.astype(BF16)
    return high, (value - high.astype(F32)).astype(BF16)


def dot(a, b):
    return jnp.dot(a, b, preferred_element_type=F32)


def dot_t(a, b):
    return lax.dot_general(a, b, (((1,), (1,)), ((), ())), preferred_element_type=F32)


def row_tile(rows):
    best = 16
    for size in range(16, 257, 16):
        if rows % size == 0:
            best = size
    return best


def planes_of(inner):
    for planes in (4, 2):
        if inner % planes == 0:
            return planes
    return 1


def kernel(
    n_inner, planes, scale,
    x_ref, cot_hbm, w_ref, mom_ref,
    ig_hbm, nw_ref, nm_ref,
    cot, xcat, xt_hi, xt_lo, wcat, s_hi, s_lo, ig, send1, recv1, send2, recv2, final, stat, stats, nw,
    cot_sem, ig_sem, ssem1, rsem1, ssem2, rsem2, ssem3, rsem3, ssem4, rsem4, ssem5,
):
    o = lax.axis_index("outer")
    i = lax.axis_index("inner")
    side = n_inner // planes
    z = i // side
    j = i % side
    rows, cin = x_ref.shape
    cout = w_ref.shape[0]
    width = cout // planes
    own = cout // n_inner
    half = cin // 2
    tile = row_tile(rows)
    tiles = rows // tile

    def plane_of(c):
        return lax.rem(z + 1 + c, planes)

    def cot_copy(c):
        k = plane_of(c)
        return pltpu.make_async_copy(
            cot_hbm.at[:, pl.ds(pl.multiple_of(k * width, width), width)], cot.at[c], cot_sem.at[c]
        )

    for c in range(planes):
        cot_copy(c).start()

    barrier = pltpu.get_barrier_semaphore()
    n_all = 2 * n_inner

    for e in range(2):

        def greet(d, _, e=e):
            @pl.when((d + e) > 0)
            def _():
                pl.semaphore_signal(
                    barrier, inc=1,
                    device_id=(lax.rem(o + e, 2), lax.rem(i + d, n_inner)), device_id_type=MESH,
                )
            return 0

        lax.fori_loop(0, n_inner, greet, 0)

    for t in range(tiles):
        at = pl.ds(t * tile, tile)
        block = x_ref[at, :]
        high, low = split(block)
        xcat[at, 0:cin] = high
        xcat[at, cin : 2 * cin] = low
        xcat[at, 2 * cin : 3 * cin] = high
        block_t = block.T
        high_t, low_t = split(block_t)
        xt_hi[t] = high_t
        xt_lo[t] = low_t
    high, low = split(w_ref[...])
    wcat[:, 0:cin] = high
    wcat[:, cin : 2 * cin] = high
    wcat[:, 2 * cin : 3 * cin] = low

    def piece_copy(c, e, d):
        other = lax.rem(o + e, 2)
        target = lax.rem(j + d, side)
        return pltpu.make_async_remote_copy(
            src_ref=send1.at[c, other, target],
            dst_ref=recv1.at[c, o, j],
            send_sem=ssem1.at[c, e, d],
            recv_sem=rsem1.at[c, o, j],
            device_id=(other, z * side + target),
            device_id_type=MESH,
        )

    def piece_arrival(c, e, d):
        g = lax.rem(o + e, 2)
        source = lax.rem(j + side - d, side)
        return pltpu.make_async_remote_copy(
            src_ref=recv1.at[c, g, source],
            dst_ref=recv1.at[c, g, source],
            send_sem=ssem1.at[c, e, d],
            recv_sem=rsem1.at[c, g, source],
            device_id=(g, z * side + source),
            device_id_type=MESH,
        )

    pieces = [(e, d) for d in range(side) for e in range(2) if (e, d) != (0, 0)]

    def plane_copy(c):
        return pltpu.make_async_remote_copy(
            src_ref=send2.at[c],
            dst_ref=recv2.at[c],
            send_sem=ssem2.at[c],
            recv_sem=rsem2.at[c],
            device_id=(o, plane_of(c) * side + j),
            device_id_type=MESH,
        )

    def gather_plane(c):
        for e, d in pieces:
            piece_arrival(c, e, d).wait_recv()
        total = recv1[c, :, 0]
        for source in range(1, side):
            total = total + recv1[c, :, source]
        return total

    def compute(c):
        k = plane_of(c)
        cot_copy(c).wait()
        w_at = pl.ds(pl.multiple_of(k * width, width), width)
        w_k = wcat[w_at, :]

        def pre_of(t):
            return dot_t(xcat[t * tile : (t + 1) * tile, :], w_k)

        pre_next = pre_of(0)
        acc = jnp.zeros((cin, width), F32)
        for t in range(tiles):
            pre = pre_next
            if t + 1 < tiles:
                pre_next = pre_of(t + 1)
            at = pl.ds(t * tile, tile)
            sig = 1.0 / (1.0 + jnp.exp(-pre))
            slope = cot[c, at, :] * (sig * (1.0 + pre * (1.0 - sig)))
            high, low = split(slope)
            s_hi[k, at, :] = high
            s_lo[k, at, :] = low
            acc = acc + (dot(xt_hi[t], high) + dot(xt_hi[t], low) + dot(xt_lo[t], high))
        grad = acc.T * scale
        for h in range(2):
            send1[c, h] = grad[:, h * half : (h + 1) * half].reshape(side, own, half)

    def chunk(c, _):
        compute(c)

        @pl.when(c == 0)
        def _():
            pl.semaphore_wait(barrier, n_all - 1)

        for e, d in pieces:
            piece_copy(c, e, d).start()
        recv1[c, o, j] = send1[c, o, j]

        @pl.when(c > 0)
        def _():
            send2[c - 1] = gather_plane(c - 1)
            plane_copy(c - 1).start()

        return 0

    lax.fori_loop(0, planes, chunk, 0)

    def input_grad(t):
        at = pl.ds(t * tile, tile)
        total = jnp.zeros((tile, cin), F32)
        for k in range(planes):
            w_at = pl.ds(k * width, width)
            w_hi = wcat[w_at, 0:cin]
            total = total + dot(s_hi[k, at, :], w_hi) + dot(s_lo[k, at, :], w_hi)
            total = total + dot(s_hi[k, at, :], wcat[w_at, 2 * cin : 3 * cin])
        ig[at, :] = total
        pltpu.make_async_copy(ig.at[at, :], ig_hbm.at[at, :], ig_sem.at[t]).start()

    early = tiles // 2 + 1
    for t in range(early):
        input_grad(t)

    total = gather_plane(planes - 1)
    for c in range(planes - 1):
        plane_copy(c).wait_recv()
        total = total + recv2[c]
    final[...] = total
    first, second = total[0], total[1]

    me = o * n_inner + i
    rows_of = [
        jnp.sum(value, axis=0, keepdims=True)
        for value in (first * second, first * first, second * second)
    ]
    stat[...] = jnp.concatenate(rows_of + [jnp.zeros((5, half), F32)], axis=0)
    stats[me] = stat[...]

    def stat_copy(e, d):
        other = lax.rem(o + e, 2)
        target = lax.rem(i + d, n_inner)
        return pltpu.make_async_remote_copy(
            src_ref=stat,
            dst_ref=stats.at[me],
            send_sem=ssem3.at[e, d],
            recv_sem=rsem3.at[me],
            device_id=(other, target),
            device_id_type=MESH,
        )

    def stat_arrival(e, d):
        g = lax.rem(o + e, 2)
        source = lax.rem(i + n_inner - d, n_inner)
        return pltpu.make_async_remote_copy(
            src_ref=stat,
            dst_ref=stats.at[g * n_inner + source],
            send_sem=ssem3.at[e, d],
            recv_sem=rsem3.at[g * n_inner + source],
            device_id=(g, source),
            device_id_type=MESH,
        )

    everybody = [(e, d) for d in range(n_inner) for e in range(2) if (e, d) != (0, 0)]
    for e, d in everybody:
        stat_copy(e, d).start()

    for t in range(early, tiles):
        input_grad(t)

    for e, d in everybody:
        stat_arrival(e, d).wait_recv()
    sums = jnp.sum(jnp.sum(stats[...], axis=0), axis=1, keepdims=True)
    cross, first_sq, second_sq = sums[0:1], sums[1:2], sums[2:3]
    combined = (1.0 - cross / (2.0 * (first_sq + 1e-06))) * final[0] + (
        1.0 - cross / (2.0 * (second_sq + 1e-06))
    ) * final[1]
    momentum = 0.9 * mom_ref[...] + combined
    nm_ref[...] = momentum
    w_rows = w_ref[pl.ds(pl.multiple_of(i * own, own), own), :]
    w_own = jnp.where(o == 0, w_rows[:, 0:half], w_rows[:, half : 2 * half])
    nw[i] = w_own - 0.1 * momentum

    def filter_copy(block, target, send_sem):
        return pltpu.make_async_remote_copy(
            src_ref=nw.at[block],
            dst_ref=nw.at[block],
            send_sem=send_sem,
            recv_sem=rsem4.at[block],
            device_id=(o, target),
            device_id_type=MESH,
        )

    for p in range(1, planes):
        filter_copy(i, lax.rem(z + p, planes) * side + j, ssem4.at[p]).start()
    order = [0]
    for p in range(1, planes // 2 + 1):
        order += [p] if p == planes - p else [p, planes - p]
    for p in order:
        block = lax.rem(z + planes - p, planes) * side + j
        if p:
            filter_copy(block, i, ssem4.at[p]).wait_recv()
        for d in range(1, side):
            filter_copy(block, z * side + lax.rem(j + d, side), ssem5.at[p, d]).start()
    for p in range(planes):
        for d in range(1, side):
            block = lax.rem(z + planes - p, planes) * side + lax.rem(j + d, side)
            filter_copy(block, i, ssem5.at[p, d]).wait_recv()
    nw_ref[...] = nw[...]

    for t in range(tiles):
        at = pl.ds(t * tile, tile)
        pltpu.make_async_copy(ig.at[at, :], ig_hbm.at[at, :], ig_sem.at[t]).wait()
    for c in range(planes):
        for e, d in pieces:
            piece_copy(c, e, d).wait_send()
        if c < planes - 1:
            plane_copy(c).wait_send()
    for e, d in everybody:
        stat_copy(e, d).wait_send()
    for p in range(planes):
        if p:
            filter_copy(i, lax.rem(z + p, planes) * side + j, ssem4.at[p]).wait_send()
        block = lax.rem(z + planes - p, planes) * side + j
        for d in range(1, side):
            filter_copy(block, z * side + lax.rem(j + d, side), ssem5.at[p, d]).wait_send()


def solution(mesh):
    n_inner = mesh.shape["inner"]
    planes = planes_of(n_inner)
    side = n_inner // planes

    def per_device(inputs, cotangent, weight, momentum):
        rows, cin = inputs.shape
        cout = weight.shape[0]
        own, half = momentum.shape
        width = cout // planes
        tile = row_tile(rows)
        tiles = rows // tile
        dma = pltpu.SemaphoreType.DMA
        vmem = pl.BlockSpec(memory_space=pltpu.VMEM)
        hbm = pl.BlockSpec(memory_space=pl.ANY)
        input_grad, new_weight, new_momentum = pl.pallas_call(
            functools.partial(kernel, n_inner, planes, 1.0 / (rows * n_inner)),
            out_shape=(
                jax.ShapeDtypeStruct((rows, cin), F32),
                jax.ShapeDtypeStruct((n_inner, own, half), F32),
                jax.ShapeDtypeStruct((own, half), F32),
            ),
            in_specs=[vmem, hbm, vmem, vmem],
            out_specs=(hbm, vmem, vmem),
            scratch_shapes=[
                pltpu.VMEM((planes, rows, width), F32),
                pltpu.VMEM((rows, 3 * cin), BF16),
                pltpu.VMEM((tiles, cin, tile), BF16),
                pltpu.VMEM((tiles, cin, tile), BF16),
                pltpu.VMEM((cout, 3 * cin), BF16),
                pltpu.VMEM((planes, rows, width), BF16),
                pltpu.VMEM((planes, rows, width), BF16),
                pltpu.VMEM((rows, cin), F32),
                pltpu.VMEM((planes, 2, side, own, half), F32),
                pltpu.VMEM((planes, 2, side, own, half), F32),
                pltpu.VMEM((planes, 2, own, half), F32),
                pltpu.VMEM((planes, 2, own, half), F32),
                pltpu.VMEM((2, own, half), F32),
                pltpu.VMEM((8, half), F32),
                pltpu.VMEM((2 * n_inner, 8, half), F32),
                pltpu.VMEM((n_inner, own, half), F32),
                dma((planes,)),
                dma((tiles,)),
                dma((planes, 2, side)),
                dma((planes, 2, side)),
                dma((planes,)),
                dma((planes,)),
                dma((2, n_inner)),
                dma((2 * n_inner,)),
                dma((planes,)),
                dma((n_inner,)),
                dma((planes, side)),
            ],
            compiler_params=pltpu.CompilerParams(
                collective_id=0, has_side_effects=True, vmem_limit_bytes=60 * 1024 * 1024
            ),
            name="adasum_step",
        )(inputs, cotangent, weight, momentum)
        return input_grad, new_weight.reshape(cout, half), new_momentum

    placed = (P(("outer", "inner"), None), P(("outer", "inner"), None), P(), P("inner", "outer"))
    return jax.shard_map(
        per_device,
        mesh=mesh,
        in_specs=placed,
        out_specs=(P(("outer", "inner"), None), P(None, "outer"), P("inner", "outer")),
        check_vma=False,
    )
```

time: 212 us -> 47.4 us (0.22)
  waiting for transfers between devices: 81.6 us -> 0 us
  blocking collectives: 77.9 us -> 0 us
  Pallas kernels: 0 us -> 42.4 us
  matrix products: 29.7 us -> 0 us
  between operations: 16.6 us -> 0.66 us
    reduce_scatter x1 -> x0, waiting for transfers between devices: 81.5 us -> none  [per_device(): lax.psum_scatter(product * scale, 'inner', scatter_dimension=0, tiled=True)]
    pallas_call x0 -> x1, Pallas kernels: none -> 42.4 us  [per_device(): pl.pallas_call(functools.partial(kernel, n_inner, planes, 1.0 / (rows * n...]
    all_gather x1 -> x0, blocking collectives: 40.1 us -> none  [per_device(): lax.all_gather(own_rows - 0.1 * new_momentum, 'inner', axis=0, tiled=True)]
    psum x1 -> x0, blocking collectives: 37.8 us -> none  [combine_level(): lax.psum((jnp.sum(shard * other), jnp.sum(shard * shard), jnp.sum(other *...]
    dot_general x3 -> x0, matrix products: 29.7 us -> none  [the longest x1 11.7 us: per_device(): lax.dot_general(slope, inputs, (((0,), (0,)), ((), ())), precision=HIGH,...]
    unnamed x11 -> x7, local copies, waits for them, and re-layouts: 4.87 us -> 4.15 us
  transfers between devices with their start and end apart: 2 -> 0, of which waited for: 1 -> 0; matrix products, arithmetic and copies ran while one was open for 4% -> 0% of each run, Pallas kernels for 0% -> 0%
where the time goes in v1:
time: 47.4 us; the launch traced here: 47.2 us
  Pallas kernels  42.4 us (89%)
  local copies, waits for them, and re-layouts  4.15 us (9%)
  between operations  0.66 us (1%)
    pallas_call x1, Pallas kernels, per_device(): pl.pallas_call(functools.partial(kernel, n_inner, planes, 1.0 / (rows * n...  42.4 us
    unnamed x7, local copies, waits for them, and re-layouts  4.15 us

profile of v1, /device:TPU:0, one launch (start us, length us, event | category | flops | bytes accessed | tf_op | source)
XLA Modules:
  0.0 47.2 jit_solution(5672102516152418944)
XLA Ops:
  0.6 42.4 %adasum_step.1 = (f32[1568,256]{1,0:T(8,128)}, f32[16,64,128]{2,1,0:T(8,128)}, f32[64,128]{1,0:T(8,128)}) custom-call(f32[1568,256]{1,0:T(8,128)} %x_ref.1, f32[1568,1024]{1,0:T(8,128)} %cot_hbm.1, f32[1024,256]{1,0:T(8,128)} %w_ref.1, f32[64,128]{1,0:T(8,128)} %mom_ref.1), custom_call_target="tpu_custom_call" | custom-call | tf_op jit(solution)/shard_map/adasum_step/pallas_call | solution.py:331
  43.0 0.0 copy-start
  43.0 0.0 copy-start.1
  43.0 2.7 %copy.10 = f32[1568,256]{1,0:T(8,128)} copy(f32[1568,256]{1,0:T(8,128)} %get-tuple-element.12) | data formatting | bytes 3211264
  45.8 0.0 copy-done
  45.8 0.8 %copy.11 = f32[1024,128]{1,0:T(8,128)} copy(f32[1024,128]{1,0:T(8,128)S(1)} %bitcast.1) | data formatting | bytes 1048576
  46.6 0.0 copy-done.1
  46.6 0.6 %copy.12 = f32[64,128]{1,0:T(8,128)} copy(f32[64,128]{1,0:T(8,128)S(1)} %copy-done.1) | data formatting | bytes 65536
Async XLA Ops:
  43.0 2.8 %copy-start = (f32[16,64,128]{2,1,0:T(8,128)S(1)}, f32[16,64,128]{2,1,0:T(8,128)}, u32[]{:S(2)}) copy-start(f32[16,64,128]{2,1,0:T(8,128)} %get-tuple-element.7) | copy-start | bytes 1572868
  43.0 3.5 %copy-start.1 = (f32[64,128]{1,0:T(8,128)S(1)}, f32[64,128]{1,0:T(8,128)}, u32[]{:S(2)}) copy-start(f32[64,128]{1,0:T(8,128)} %get-tuple-element.14) | copy-start | bytes 98308

commit v2 on v1

--- a/solution.py
+++ b/solution.py
@@ -43,9 +43,9 @@
 def kernel(
     n_inner, planes, scale,
     x_ref, cot_hbm, w_ref, mom_ref,
-    ig_hbm, nw_ref, nm_ref,
-    cot, xcat, xt_hi, xt_lo, wcat, s_hi, s_lo, ig, send1, recv1, send2, recv2, final, stat, stats, nw,
-    cot_sem, ig_sem, ssem1, rsem1, ssem2, rsem2, ssem3, rsem3, ssem4, rsem4, ssem5,
+    ig, nw_ref, nm_ref,
+    cot, xcat, xt_hi, xt_lo, wcat, s_hi, s_lo, send1, recv1, send2, recv2, raw, moms, stat, stats, nw,
+    cot_sem, ssem1, rsem1, ssem2, rsem2, ssem3, rsem3, ssem4, rsem4, ssem5, rsem5, ssem6, rsem6, ssem7, rsem7,
 ):
     o = lax.axis_index("outer")
     i = lax.axis_index("inner")
@@ -147,6 +147,29 @@
         for source in range(1, side):
             total = total + recv1[c, :, source]
         return total
+
+    def line_copy(array, p, ssem, rsem):
+        return pltpu.make_async_remote_copy(
+            src_ref=array.at[z],
+            dst_ref=array.at[z],
+            send_sem=ssem.at[p],
+            recv_sem=rsem.at[z],
+            device_id=(o, lax.rem(z + p, planes) * side + j),
+            device_id_type=MESH,
+        )
+
+    def line_arrival(array, p, ssem, rsem):
+        source = lax.rem(z + planes - p, planes)
+        return pltpu.make_async_remote_copy(
+            src_ref=array.at[source],
+            dst_ref=array.at[source],
+            send_sem=ssem.at[p],
+            recv_sem=rsem.at[source],
+            device_id=(o, source * side + j),
+            device_id_type=MESH,
+        )
+
+    moms[z] = mom_ref[...]
 
     def compute(c):
         k = plane_of(c)
@@ -185,6 +208,11 @@
             piece_copy(c, e, d).start()
         recv1[c, o, j] = send1[c, o, j]
 
+        @pl.when(c == 0)
+        def _():
+            for p in range(1, planes):
+                line_copy(moms, p, ssem6, rsem6).start()
+
         @pl.when(c > 0)
         def _():
             send2[c - 1] = gather_plane(c - 1)
@@ -203,7 +231,6 @@
             total = total + dot(s_hi[k, at, :], w_hi) + dot(s_lo[k, at, :], w_hi)
             total = total + dot(s_hi[k, at, :], wcat[w_at, 2 * cin : 3 * cin])
         ig[at, :] = total
-        pltpu.make_async_copy(ig.at[at, :], ig_hbm.at[at, :], ig_sem.at[t]).start()
 
     early = tiles // 2 + 1
     for t in range(early):
@@ -213,7 +240,7 @@
     for c in range(planes - 1):
         plane_copy(c).wait_recv()
         total = total + recv2[c]
-    final[...] = total
+    raw[z] = total
     first, second = total[0], total[1]
 
     me = o * n_inner + i
@@ -251,6 +278,8 @@
     everybody = [(e, d) for d in range(n_inner) for e in range(2) if (e, d) != (0, 0)]
     for e, d in everybody:
         stat_copy(e, d).start()
+    for p in range(1, planes):
+        line_copy(raw, p, ssem4, rsem5).start()
 
     for t in range(early, tiles):
         input_grad(t)
@@ -259,45 +288,84 @@
         stat_arrival(e, d).wait_recv()
     sums = jnp.sum(jnp.sum(stats[...], axis=0), axis=1, keepdims=True)
     cross, first_sq, second_sq = sums[0:1], sums[1:2], sums[2:3]
-    combined = (1.0 - cross / (2.0 * (first_sq + 1e-06))) * final[0] + (
-        1.0 - cross / (2.0 * (second_sq + 1e-06))
-    ) * final[1]
-    momentum = 0.9 * mom_ref[...] + combined
-    nm_ref[...] = momentum
-    w_rows = w_ref[pl.ds(pl.multiple_of(i * own, own), own), :]
-    w_own = jnp.where(o == 0, w_rows[:, 0:half], w_rows[:, half : 2 * half])
-    nw[i] = w_own - 0.1 * momentum
-
-    def filter_copy(block, target, send_sem):
-        return pltpu.make_async_remote_copy(
-            src_ref=nw.at[block],
-            dst_ref=nw.at[block],
+    first_by = 1.0 - cross / (2.0 * (first_sq + 1e-06))
+    second_by = 1.0 - cross / (2.0 * (second_sq + 1e-06))
+
+    def filter_copy(block, at, target, send_sem, recv_sem):
+        return pltpu.make_async_remote_copy(
+            src_ref=nw.at[block, at],
+            dst_ref=nw.at[block, at],
             send_sem=send_sem,
-            recv_sem=rsem4.at[block],
-            device_id=(o, target),
-            device_id_type=MESH,
-        )
-
-    for p in range(1, planes):
-        filter_copy(i, lax.rem(z + p, planes) * side + j, ssem4.at[p]).start()
+            recv_sem=recv_sem,
+            device_id=(o, z * side + target),
+            device_id_type=MESH,
+        )
+
+    def plane_back(p):
+        return lax.rem(z + planes - p, planes)
+
+    whole = pl.ds(0, own)
+    square = side == 4 and own % 16 == 0
+    across = j + 1 - 2 * lax.rem(j, 2)
+    along = j + 2 - 4 * (j // 2)
+    targets = (across, along) if square else tuple(lax.rem(j + d, side) for d in range(1, side))
+    sources = targets if square else tuple(lax.rem(j + side - d, side) for d in range(1, side))
+    low_rows, high_rows = pl.ds(0, own // 2), pl.ds(own // 2, own // 2)
+
+    def block_copies(p):
+        block = plane_back(p) * side + j
+        return [
+            filter_copy(block, whole, target, ssem5.at[p, d], rsem4.at[block])
+            for d, target in enumerate(targets)
+        ]
+
+    def block_arrival(p, d):
+        block = plane_back(p) * side + sources[d]
+        return filter_copy(block, whole, j, ssem5.at[p, d], rsem4.at[block])
+
+    def forward_copies(p):
+        q = plane_back(p)
+        return [
+            filter_copy(q * side + across, low_rows, along, ssem7.at[p, 0], rsem7.at[q, 0]),
+            filter_copy(q * side + along, high_rows, across, ssem7.at[p, 1], rsem7.at[q, 1]),
+        ]
+
+    def forward(p):
+        for d, copy in enumerate(forward_copies(p)):
+            block_arrival(p, d).wait_recv()
+            copy.start()
+
     order = [0]
     for p in range(1, planes // 2 + 1):
         order += [p] if p == planes - p else [p, planes - p]
+    for at, p in enumerate(order):
+        q = plane_back(p)
+        if p:
+            line_arrival(moms, p, ssem6, rsem6).wait_recv()
+            line_arrival(raw, p, ssem4, rsem5).wait_recv()
+        momentum = 0.9 * moms[q] + (first_by * raw[q, 0] + second_by * raw[q, 1])
+        if p == 0:
+            nm_ref[...] = momentum
+        block = q * side + j
+        w_rows = w_ref[pl.ds(pl.multiple_of(block * own, own), own), :]
+        w_own = jnp.where(o == 0, w_rows[:, 0:half], w_rows[:, half : 2 * half])
+        nw[block] = w_own - 0.1 * momentum
+        for copy in block_copies(p):
+            copy.start()
+        if square and at:
+            forward(order[at - 1])
+    if square:
+        forward(order[-1])
     for p in order:
-        block = lax.rem(z + planes - p, planes) * side + j
-        if p:
-            filter_copy(block, i, ssem4.at[p]).wait_recv()
-        for d in range(1, side):
-            filter_copy(block, z * side + lax.rem(j + d, side), ssem5.at[p, d]).start()
-    for p in range(planes):
-        for d in range(1, side):
-            block = lax.rem(z + planes - p, planes) * side + lax.rem(j + d, side)
-            filter_copy(block, i, ssem5.at[p, d]).wait_recv()
+        q = plane_back(p)
+        if square:
+            for d, at in enumerate((low_rows, high_rows)):
+                filter_copy(q * side + (side - 1 - j), at, j, ssem7.at[p, d], rsem7.at[q, d]).wait_recv()
+        else:
+            for d in range(len(sources)):
+                block_arrival(p, d).wait_recv()
     nw_ref[...] = nw[...]
 
-    for t in range(tiles):
-        at = pl.ds(t * tile, tile)
-        pltpu.make_async_copy(ig.at[at, :], ig_hbm.at[at, :], ig_sem.at[t]).wait()
     for c in range(planes):
         for e, d in pieces:
             piece_copy(c, e, d).wait_send()
@@ -307,10 +375,24 @@
         stat_copy(e, d).wait_send()
     for p in range(planes):
         if p:
-            filter_copy(i, lax.rem(z + p, planes) * side + j, ssem4.at[p]).wait_send()
-        block = lax.rem(z + planes - p, planes) * side + j
-        for d in range(1, side):
-            filter_copy(block, z * side + lax.rem(j + d, side), ssem5.at[p, d]).wait_send()
+            line_copy(moms, p, ssem6, rsem6).wait_send()
+            line_copy(raw, p, ssem4, rsem5).wait_send()
+        for copy in block_copies(p):
+            copy.wait_send()
+        if square:
+            for copy in forward_copies(p):
+                copy.wait_send()
+
+
+def store_kernel(a, b, c, a_out, b_out, c_out, sems):
+    copies = [
+        pltpu.make_async_copy(source, target, sems.at[n])
+        for n, (source, target) in enumerate(((a, a_out), (b, b_out), (c, c_out)))
+    ]
+    for copy in copies:
+        copy.start()
+    for copy in copies:
+        copy.wait()
 
 
 def solution(mesh):
@@ -331,12 +413,12 @@
         input_grad, new_weight, new_momentum = pl.pallas_call(
             functools.partial(kernel, n_inner, planes, 1.0 / (rows * n_inner)),
             out_shape=(
-                jax.ShapeDtypeStruct((rows, cin), F32),
-                jax.ShapeDtypeStruct((n_inner, own, half), F32),
-                jax.ShapeDtypeStruct((own, half), F32),
+                pltpu.VMEM((rows, cin), F32),
+                pltpu.VMEM((n_inner, own, half), F32),
+                pltpu.VMEM((own, half), F32),
             ),
             in_specs=[vmem, hbm, vmem, vmem],
-            out_specs=(hbm, vmem, vmem),
+            out_specs=(vmem, vmem, vmem),
             scratch_shapes=[
                 pltpu.VMEM((planes, rows, width), F32),
                 pltpu.VMEM((rows, 3 * cin), BF16),
@@ -345,17 +427,16 @@
                 pltpu.VMEM((cout, 3 * cin), BF16),
                 pltpu.VMEM((planes, rows, width), BF16),
                 pltpu.VMEM((planes, rows, width), BF16),
-                pltpu.VMEM((rows, cin), F32),
                 pltpu.VMEM((planes, 2, side, own, half), F32),
                 pltpu.VMEM((planes, 2, side, own, half), F32),
                 pltpu.VMEM((planes, 2, own, half), F32),
                 pltpu.VMEM((planes, 2, own, half), F32),
-                pltpu.VMEM((2, own, half), F32),
+                pltpu.VMEM((planes, 2, own, half), F32),
+                pltpu.VMEM((planes, own, half), F32),
                 pltpu.VMEM((8, half), F32),
                 pltpu.VMEM((2 * n_inner, 8, half), F32),
                 pltpu.VMEM((n_inner, own, half), F32),
                 dma((planes,)),
-                dma((tiles,)),
                 dma((planes, 2, side)),
                 dma((planes, 2, side)),
                 dma((planes,)),
@@ -365,12 +446,28 @@
                 dma((planes,)),
                 dma((n_inner,)),
                 dma((planes, side)),
+                dma((planes,)),
+                dma((planes,)),
+                dma((planes,)),
+                dma((planes, 2)),
+                dma((planes, 2)),
             ],
             compiler_params=pltpu.CompilerParams(
-                collective_id=0, has_side_effects=True, vmem_limit_bytes=60 * 1024 * 1024
+                collective_id=0, has_side_effects=True, vmem_limit_bytes=56 * 1024 * 1024
             ),
             name="adasum_step",
         )(inputs, cotangent, weight, momentum)
+        input_grad, new_weight, new_momentum = pl.pallas_call(
+            store_kernel,
+            out_shape=tuple(
+                jax.ShapeDtypeStruct(value.shape, F32) for value in (input_grad, new_weight, new_momentum)
+            ),
+            in_specs=[vmem] * 3,
+            out_specs=(hbm, hbm, hbm),
+            scratch_shapes=[dma((3,))],
+            compiler_params=pltpu.CompilerParams(vmem_limit_bytes=4 * 1024 * 1024),
+            name="store_results",
+        )(input_grad, new_weight, new_momentum)
         return input_grad, new_weight.reshape(cout, half), new_momentum
 
     placed = (P(("outer", "inner"), None), P(("outer", "inner"), None), P(), P("inner", "outer"))

time: 47.4 us -> 45.6 us (0.962)
  local copies, waits for them, and re-layouts: 4.15 us -> 0 us
  Pallas kernels: 42.4 us -> 44.8 us
    unnamed x7 -> x0, local copies, waits for them, and re-layouts: 4.15 us -> none
    pallas_call x0 -> x1, Pallas kernels: none -> 1.35 us  [per_device(): pl.pallas_call(store_kernel, out_shape=tuple((jax.ShapeDtypeStruct(value....]
    pallas_call x1, Pallas kernels: 42.4 us -> 43.4 us  [per_device(): pl.pallas_call(functools.partial(kernel, n_inner, planes, 1.0 / (rows * n...]
where the time goes in v2:
time: 45.6 us; the launch traced here: 45.4 us
  Pallas kernels  44.8 us (98%)
  between operations  0.64 us (1%)
    pallas_call x1, Pallas kernels, per_device(): pl.pallas_call(functools.partial(kernel, n_inner, planes, 1.0 / (rows * n...  43.4 us
    pallas_call x1, Pallas kernels, per_device(): pl.pallas_call(store_kernel, out_shape=tuple((jax.ShapeDtypeStruct(value....  1.35 us

profile of v2, /device:TPU:0, one launch (start us, length us, event | category | flops | bytes accessed | tf_op | source)
XLA Modules:
  0.0 45.4 jit_solution(15637356566061740401)
XLA Ops:
  0.6 43.4 %adasum_step.1 = (f32[1568,256]{1,0:T(8,128)S(1)}, f32[16,64,128]{2,1,0:T(8,128)S(1)}, f32[64,128]{1,0:T(8,128)S(1)}) custom-call(f32[1568,256]{1,0:T(8,128)} %x_ref.1, f32[1568,1024]{1,0:T(8,128)} %cot_hbm.1, f32[1024,256]{1,0:T(8,128)} %w_ref.1, f32[64,128]{1,0:T(8,128)} %mom_ref.1), custom_call_target="tpu_custom_call" | custom-call | tf_op jit(solution)/shard_map/adasum_step/pallas_call | solution.py:413
  44.1 1.4 %store_results.1 = (f32[1568,256]{1,0:T(8,128)}, f32[16,64,128]{2,1,0:T(8,128)}, f32[64,128]{1,0:T(8,128)}) custom-call(f32[1568,256]{1,0:T(8,128)S(1)} %get-tuple-element.9.a, f32[16,64,128]{2,1,0:T(8,128)S(1)} %get-tuple-element.10.b, f32[64,128]{1,0:T(8,128)S(1)} %get-tuple-element.11.c), custom_call_target="tpu_custom_call" | custom-call | tf_op jit(solution)/shard_map/store_results/pallas_call | solution.py:460

commit v3 on v2

--- a/solution.py
+++ b/solution.py
@@ -170,6 +170,8 @@
         )
 
     moms[z] = mom_ref[...]
+    far = planes // 2 if planes > 2 and planes % 2 == 0 else 0
+    near = [p for p in range(1, planes) if p != far]
 
     def compute(c):
         k = plane_of(c)
@@ -210,7 +212,7 @@
 
         @pl.when(c == 0)
         def _():
-            for p in range(1, planes):
+            for p in near:
                 line_copy(moms, p, ssem6, rsem6).start()
 
         @pl.when(c > 0)
@@ -278,7 +280,7 @@
     everybody = [(e, d) for d in range(n_inner) for e in range(2) if (e, d) != (0, 0)]
     for e, d in everybody:
         stat_copy(e, d).start()
-    for p in range(1, planes):
+    for p in near:
         line_copy(raw, p, ssem4, rsem5).start()
 
     for t in range(early, tiles):
@@ -298,6 +300,16 @@
             send_sem=send_sem,
             recv_sem=recv_sem,
             device_id=(o, z * side + target),
+            device_id_type=MESH,
+        )
+
+    def far_copy(block):
+        return pltpu.make_async_remote_copy(
+            src_ref=nw.at[block],
+            dst_ref=nw.at[block],
+            send_sem=ssem4.at[far],
+            recv_sem=rsem4.at[block],
+            device_id=(o, lax.rem(z + far, planes) * side + j),
             device_id_type=MESH,
         )
 
@@ -340,16 +352,21 @@
         order += [p] if p == planes - p else [p, planes - p]
     for at, p in enumerate(order):
         q = plane_back(p)
-        if p:
-            line_arrival(moms, p, ssem6, rsem6).wait_recv()
-            line_arrival(raw, p, ssem4, rsem5).wait_recv()
-        momentum = 0.9 * moms[q] + (first_by * raw[q, 0] + second_by * raw[q, 1])
-        if p == 0:
-            nm_ref[...] = momentum
         block = q * side + j
-        w_rows = w_ref[pl.ds(pl.multiple_of(block * own, own), own), :]
-        w_own = jnp.where(o == 0, w_rows[:, 0:half], w_rows[:, half : 2 * half])
-        nw[block] = w_own - 0.1 * momentum
+        if p and p == far:
+            far_copy(block).wait_recv()
+        else:
+            if p:
+                line_arrival(moms, p, ssem6, rsem6).wait_recv()
+                line_arrival(raw, p, ssem4, rsem5).wait_recv()
+            momentum = 0.9 * moms[q] + (first_by * raw[q, 0] + second_by * raw[q, 1])
+            if p == 0:
+                nm_ref[...] = momentum
+            w_rows = w_ref[pl.ds(pl.multiple_of(block * own, own), own), :]
+            w_own = jnp.where(o == 0, w_rows[:, 0:half], w_rows[:, half : 2 * half])
+            nw[block] = w_own - 0.1 * momentum
+        if p == 0 and far:
+            far_copy(block).start()
         for copy in block_copies(p):
             copy.start()
         if square and at:
@@ -374,7 +391,9 @@
     for e, d in everybody:
         stat_copy(e, d).wait_send()
     for p in range(planes):
-        if p:
+        if p and p == far:
+            far_copy(i).wait_send()
+        elif p:
             line_copy(moms, p, ssem6, rsem6).wait_send()
             line_copy(raw, p, ssem4, rsem5).wait_send()
         for copy in block_copies(p):

time: 45.6 us -> 45.5 us (level)
  no operation moved by 1% of the time
where the time goes in v3:
time: 45.5 us; the launch traced here: 45.4 us
  Pallas kernels  44.7 us (98%)
  between operations  0.64 us (1%)
    pallas_call x1, Pallas kernels, per_device(): pl.pallas_call(functools.partial(kernel, n_inner, planes, 1.0 / (rows * n...  43.4 us
    pallas_call x1, Pallas kernels, per_device(): pl.pallas_call(store_kernel, out_shape=tuple((jax.ShapeDtypeStruct(value....  1.35 us

profile of v3, /device:TPU:0, one launch (start us, length us, event | category | flops | bytes accessed | tf_op | source)
XLA Modules:
  0.0 45.4 jit_solution(5423210273041625586)
XLA Ops:
  0.6 43.4 %adasum_step.1 = (f32[1568,256]{1,0:T(8,128)S(1)}, f32[16,64,128]{2,1,0:T(8,128)S(1)}, f32[64,128]{1,0:T(8,128)S(1)}) custom-call(f32[1568,256]{1,0:T(8,128)} %x_ref.1, f32[1568,1024]{1,0:T(8,128)} %cot_hbm.1, f32[1024,256]{1,0:T(8,128)} %w_ref.1, f32[64,128]{1,0:T(8,128)} %mom_ref.1), custom_call_target="tpu_custom_call" | custom-call | tf_op jit(solution)/shard_map/adasum_step/pallas_call | solution.py:432
  44.0 1.4 %store_results.1 = (f32[1568,256]{1,0:T(8,128)}, f32[16,64,128]{2,1,0:T(8,128)}, f32[64,128]{1,0:T(8,128)}) custom-call(f32[1568,256]{1,0:T(8,128)S(1)} %get-tuple-element.9.a, f32[16,64,128]{2,1,0:T(8,128)S(1)} %get-tuple-element.10.b, f32[64,128]{1,0:T(8,128)S(1)} %get-tuple-element.11.c), custom_call_target="tpu_custom_call" | custom-call | tf_op jit(solution)/shard_map/store_results/pallas_call | solution.py:479
